TPU v7x, 256 devices: a whole 4x4x8 slice. The times are simulated.
256 devices in a mesh: samp: 64 (over y, z, core), gene: 4 (over x).
Axes of the slice: x: 4, y: 4, z: 8, core: 2. Of those that a mesh axis runs over, the one named last changes fastest.
Arguments:
- genotypes: int32 [2048, 32768], P('samp', 'gene'), may hold values from -2147483648 to 1789569706, as said below
- allele_freq: float32 [32768], P('gene'), may hold values from 0.035 to 0.56
- sample_weight: float32 [16, 2048], P(None, 'samp'), may hold values from 0.2 to 2
- residual: float32 [16, 2048], P(None, 'samp'), may hold values from -12 to 12
- variant_weight: float32 [32768], P('gene'), may hold values from 0.2 to 4
- block_gene: int32 [256], replicated, may hold values from 0 to 127, as said below
- gene_variants: int32 [128], replicated, may hold values from 1 to 384, as said below
Outputs:
- burden_z: float32 [128], replicated
- skat_z: float32 [128], replicated
Inputs may be any that keep to these rules, and one draw needn't show every extreme that they name: Each word holds 16 dosages 0, 1 or 2: bits 2k and 2k+1 of genotypes[i, v] are the dosage of variant slot v in sample (k, i); a dosage 2 in the top field sets the sign bit. `block_gene`: never falling; the blocks come in aligned groups of four, each shared by two consecutive genes, so every gene has 1 to 3 blocks. `gene_variants`: A gene with m blocks has from (m - 1) * 128 + 1 to m * 128 live variants; the slots after them in its last block are padding.
All inputs are finite; a program needn't handle non-finite values.
Results may differ from a plain program's by a relative error of at most 0.0037.
Values sent between devices are 32-bit elements; how exact they have to be, the bound alone decides.
A program may use at most 64 MiB of HBM per device.

v0:
```python
import jax
import jax.numpy as jnp
from jax import lax
from jax.sharding import Mesh
from jax.sharding import PartitionSpec as P

BLK = 128
SAMP = ("samp_0", "samp_1", "samp_2")
SAMP_GENE = ("samp_0", "samp_1", "samp_2", "gene")


def turned_gather(arrays, axis, dims):
    turned = [jnp.moveaxis(a, dim, 0) for a, dim in zip(arrays, dims)]
    both = jnp.concatenate([t.reshape(len(t), -1) for t in turned], axis=1)
    result, at, done = (lax.all_gather(both, axis, axis=0, tiled=True), 0, [])
    for t, dim in zip(turned, dims):
        share = result[:, at : at + t[0].size].reshape(-1, *t.shape[1:])
        done.append(jnp.moveaxis(share, 0, dim))
        at += t[0].size
    return tuple(done)


def by_axis(array, axes):
    for axis in axes:
        array = lax.psum(array, axis)
    return array


def unpack(packed_words, allele_part, root_weight):
    fields = root_weight.shape[0]
    offsets = 2 * jnp.arange(fields, dtype=jnp.int32)
    dosage = jnp.bitwise_and(jnp.right_shift(packed_words[None, :, :], offsets[:, None, None]), 3)
    centered = dosage.astype(jnp.float32) - 2.0 * allele_part[None, None, :]
    return (root_weight[:, :, None] * centered).astype(jnp.bfloat16)


def block_grams(scaled, block_count):
    stacked = scaled.reshape(scaled.shape[0] * scaled.shape[1], block_count, BLK)
    return jnp.einsum("sbu,sbv->buv", stacked, stacked, preferred_element_type=jnp.float32)


def block_stats(gram_part, scores, effective):
    weighted_score = effective * scores
    burden_sum = jnp.sum(weighted_score, axis=1)
    skat_sum = jnp.sum(weighted_score * weighted_score, axis=1)
    image = jnp.einsum("buv,bv->bu", gram_part, effective)
    burden_var = jnp.sum(effective * image, axis=1)
    diagonal = jnp.diagonal(gram_part, axis1=1, axis2=2)
    trace_one = jnp.sum(effective * effective * diagonal, axis=1)
    scaled_gram = effective[:, :, None] * gram_part * effective[:, None, :]
    trace_two = jnp.sum(scaled_gram * scaled_gram, axis=(1, 2))
    return jnp.stack([burden_sum, burden_var, skat_sum, trace_one, trace_two])


def live_weights(block_ids, variant_part, block_gene, gene_variants):
    total_blocks = block_gene.shape[0]
    genes = gene_variants.shape[0]
    chosen = block_ids[:, None] == jnp.arange(total_blocks, dtype=jnp.int32)[None, :]
    gene_of = jnp.sum(jnp.where(chosen, block_gene[None, :], 0), axis=1)
    first_block = jnp.sum((block_gene[None, :] < gene_of[:, None]).astype(jnp.int32), axis=1)
    member = gene_of[:, None] == jnp.arange(genes, dtype=jnp.int32)[None, :]
    counted = jnp.sum(jnp.where(member, gene_variants[None, :], 0), axis=1)
    column = jnp.arange(BLK, dtype=jnp.int32)
    is_live = (block_ids - first_block)[:, None] * BLK + column[None, :] < counted[:, None]
    return (variant_part * is_live.astype(jnp.float32), member.astype(jnp.float32))


def local(
    genotypes, allele_freq, sample_weight, residual, variant_weight, block_gene, gene_variants
):
    local_blocks = genotypes.shape[1] // BLK
    owned_count = local_blocks // lax.axis_size(SAMP)
    samp_index = lax.axis_index(SAMP)
    gene_index = lax.axis_index("gene")
    block_ids = (
        gene_index * local_blocks
        + samp_index * owned_count
        + jnp.arange(owned_count, dtype=jnp.int32)
    )
    variant_blocks = variant_weight.reshape(local_blocks, BLK)
    own_weights = lax.dynamic_slice_in_dim(variant_blocks, samp_index * owned_count, owned_count, 0)
    effective, member = live_weights(block_ids, own_weights, block_gene, gene_variants)
    own_words = lax.all_to_all(genotypes, SAMP, split_axis=1, concat_axis=0, tiled=True)
    all_weight, all_residual = turned_gather((sample_weight, residual), SAMP, (1, 1))
    own_freq = lax.dynamic_slice_in_dim(
        allele_freq, samp_index * owned_count * BLK, owned_count * BLK, 0
    )
    root_all = jnp.sqrt(all_weight)
    weighted_residual = (root_all * all_residual).astype(jnp.bfloat16)
    scaled = unpack(own_words, own_freq, root_all)
    gram_part = block_grams(scaled, owned_count)
    flattened = scaled.reshape(scaled.shape[0] * scaled.shape[1], owned_count * BLK)
    scores = jnp.dot(
        weighted_residual.reshape(1, -1), flattened, preferred_element_type=jnp.float32
    )
    variance = jnp.sum(all_weight * all_residual * all_residual) / (
        all_weight.shape[0] * all_weight.shape[1]
    )
    gene_parts = jnp.dot(block_stats(gram_part, scores, effective), member)
    totals = by_axis(gene_parts, SAMP_GENE)
    burden = totals[0] / jnp.sqrt(variance * totals[1])
    skat_score = (totals[2] - variance * totals[3]) / (variance * jnp.sqrt(2.0 * totals[4]))
    return (burden, skat_score)


def solution(mesh):
    torus = Mesh(
        mesh.devices.reshape(4, 8, 2, mesh.shape["gene"]), ("samp_0", "samp_1", "samp_2", "gene")
    )
    placed = (P(SAMP, "gene"), P("gene"), P(None, SAMP), P(None, SAMP), P("gene"), P(), P())
    return jax.shard_map(local, mesh=torus, in_specs=placed, out_specs=(P(), P()), check_vma=False)
```

profile of v0, /device:TPU:8, one launch (start us, length us, event | category | flops | bytes accessed | tf_op | source)
XLA Modules:
  0.0 156.2 jit_solution(2203239968844073498)
XLA Ops:
  0.6 0.0 copy-start
  0.6 0.0 copy-start.1
  0.7 1.2 copy-done
  1.9 1.1 copy_bitcast_fusion
  3.0 12.1 %all-to-all-start = ((s32[32,64,128]{2,0,1:T(8,128)}), s32[32,64,128]{2,0,1:T(8,128)S(1)}, u32[]{:S(2)}, u32[]{:S(2)}) async-start(s32[32,64,128]{2,0,1:T(8,128)} %copy_bitcast_fusion), calls=%async_computation | async-start | bytes 2097152 | tf_op jit(solution)/shard_map/all_to_all | solution.py:83
  15.1 1.3 fusion.19
  16.4 2.0 %fusion.20 = s32[]{:T(128)} fusion(s32[256]{0:T(256)} %param.12, s32[]{:T(128)} %fusion.19), kind=kLoop, calls=%fused_computation.36 | loop fusion | flops 767 | bytes 1032 | tf_op jit(solution)/shard_map/reduce_sum | solution.py:60
  19.1 0.8 copy.15
  19.8 0.8 copy.16
  20.6 0.1 pad_maximum_fusion
  20.7 62.9 %all_gather.3 = f32[2048,32]{1,0:T(8,128)S(1)} all-gather(f32[32,32]{1,0:T(8,128)S(1)} %pad_maximum_fusion), channel_id=1, replica_groups=mesh['samp_0'=4,'samp_1'=8,'samp_2'=2,'gene'=4] {'samp_0','samp_1','samp..., dimensions={0}, use_global_device_ids=true | all-gather | bytes 266240 | tf_op jit(solution)/shard_map/all_gather | solution.py:15
  83.6 1.9 %fusion.15 = (f32[]{:T(128)}, bf16[16,2048,1]{0,1,2:T(8,128)(2,1)}, f32[16,2048]{0,1:T(8,128)S(1)}) fusion(f32[2048,32]{1,0:T(8,128)S(1)} %all_gather.3), kind=kLoop, calls=%fused_computation.19 | loop fusion | flops 163839 | bytes 458756 | tf_op jit(solution)/shard_map/reduce_sum | solution.py:96
  85.5 1.4 copy.21
  86.9 0.3 copy.17
  87.8 0.7 fusion.22
  88.5 0.8 dynamic-slice_multiply_fusion
  89.3 0.0 copy-done.1
  89.3 1.3 fusion.21
  90.6 0.0 all-to-all-done
  90.6 0.3 copy.19
  90.9 6.6 %multiply_convert_fusion.14 = bf16[16,2048,128]{1,2,0:T(8,128)(2,1)} fusion(f32[128]{0:T(128)S(1)} %dynamic-slice_multiply_fusion, s32[16]{0:T(128)S(1)} %iota_multiply_fusion, s32[2048,128]{0,1:T(8,128)S(1)} %copy.19, f32[16,2048]{1,0:T(8,128)S(1)} %copy.17), kind=kLoop, calls=%fused_computation.1.clone.clone.clone.clone.2 | loop fusion | flops 25165824 | bytes 9568832 | tf_op jit(solution)/shard_map/sbu,sbv->buv/dot_general | solution.py:39
  97.5 8.1 %fusion.12 = f32[128,128]{1,0:T(8,128)S(1)} fusion(bf16[16,2048,128]{1,2,0:T(8,128)(2,1)} %multiply_convert_fusion.14), kind=kOutput, calls=%fused_computation.15 | convolution fusion | flops 1073741824 | bytes 8454144 | tf_op jit(solution)/shard_map/sbu,sbv->buv/dot_general | solution.py:39
  105.6 1.4 gather_fusion
  107.0 1.9 %fusion.23 = (f32[]{:T(128)}, f32[1,128]{1,0:T(1,128)S(1)}) fusion(f32[128]{0:T(128)S(1)} %gather_fusion, f32[64,128]{1,0:T(8,128)} %bitcast.70, s32[]{:T(128)S(6)} %select_n.22, s32[]{:T(128)} %fusion.21, s32[]{:T(128)S(6)} %mul.117), kind=kLoop, calls=%fused_computation.40 | loop fusion | flops 767 | bytes 1552 | tf_op jit(solution)/shard_map/reduce_sum | solution.py:49
  109.0 0.7 fusion.17
  109.7 3.9 %multiply_reduce_fusion.1 = (f32[]{:T(128)}, f32[]{:T(128)}) fusion(f32[1,128]{1,0:T(1,128)S(1)} %get-tuple-element.5, bf16[16,2048,1]{1,2,0:T(2,128)(2,1)S(1)} %copy.21, f32[128]{0:T(128)S(1)} %dynamic-slice_multiply_fusion, s32[16]{0:T(128)S(1)} %iota_multiply_fusion, s32[2048,128]{0,1:T(8,128)S(1)} %copy.19, f32[16,2048]{1,0:T(8,128)S(1)} %copy.17), kind=kOutput, calls=%fused_computation.45 | convolution fusion | flops 33554944 | bytes 1246280 | tf_op jit(solution)/shard_map/dot_general | solution.py:93
  113.6 0.7 multiply_reduce_fusion
  114.3 3.3 %stack.23 = f32[5,1]{0,1:T(1,128)S(1)} concatenate(f32[1,1]{0,1:T(1,128)} %bitcast.10, f32[1,1]{0,1:T(1,128)} %bitcast.15, f32[1,1]{0,1:T(1,128)} %bitcast.16, f32[1,1]{0,1:T(1,128)} %bitcast.19, f32[1,1]{0,1:T(1,128)} %bitcast.20), dimensions={0} | concatenate | bytes 40 | tf_op jit(solution)/shard_map/stack | solution.py:52
  117.6 0.1 broadcast_multiply_fusion
  117.7 8.6 %psum.28 = f32[5,128]{1,0:T(8,128)S(1)} all-reduce(f32[5,128]{1,0:T(8,128)S(1)} %broadcast_multiply_fusion), channel_id=1, replica_groups=mesh['samp_0'=4,'samp_1'=8,'samp_2'=2,'gene'=4] {'samp_0'}, use_global_device_ids=true, to_apply=%region_8.9 | all-reduce | flops 640 | bytes 5120 | tf_op jit(solution)/shard_map/psum | solution.py:25
  126.2 16.5 %psum.29 = f32[5,128]{1,0:T(8,128)S(1)} all-reduce(f32[5,128]{1,0:T(8,128)S(1)} %psum.28), channel_id=1, replica_groups=mesh['samp_0'=4,'samp_1'=8,'samp_2'=2,'gene'=4] {'samp_1'}, use_global_device_ids=true, to_apply=%region_9.10 | all-reduce | flops 640 | bytes 5120 | tf_op jit(solution)/shard_map/psum | solution.py:25
  142.8 2.5 %psum.30 = f32[5,128]{1,0:T(8,128)S(1)} all-reduce(f32[5,128]{1,0:T(8,128)S(1)} %psum.29), channel_id=1, replica_groups=mesh['samp_0'=4,'samp_1'=8,'samp_2'=2,'gene'=4] {'samp_2'}, use_global_device_ids=true, to_apply=%region_10.11 | all-reduce | flops 640 | bytes 5120 | tf_op jit(solution)/shard_map/psum | solution.py:25
  145.2 10.5 %psum.31 = f32[5,128]{1,0:T(8,128)S(1)} all-reduce(f32[5,128]{1,0:T(8,128)S(1)} %psum.30), channel_id=1, replica_groups=mesh['samp_0'=4,'samp_1'=8,'samp_2'=2,'gene'=4] {'gene'}, use_global_device_ids=true, to_apply=%region_11.12 | all-reduce | flops 640 | bytes 5120 | tf_op jit(solution)/shard_map/psum | solution.py:25
  155.7 0.5 fusion.25
  (2 shorter events, 0.0 us)
Async XLA Ops:
  0.6 1.2 copy-start
  0.6 88.6 %copy-start.1 = (s32[128]{0:T(128)S(1)}, s32[128]{0:T(128)}, u32[]{:S(2)}) copy-start(s32[128]{0:T(128)} %param.13) | copy-start | bytes 1540
  3.0 87.6 %all-to-all-start = ((s32[32,64,128]{2,0,1:T(8,128)}), s32[32,64,128]{2,0,1:T(8,128)S(1)}, u32[]{:S(2)}, u32[]{:S(2)}) async-start(s32[32,64,128]{2,0,1:T(8,128)} %copy_bitcast_fusion), calls=%async_computation | async-start | bytes 2097152 | tf_op jit(solution)/shard_map/all_to_all | solution.py:83
where the time goes:
time: 157 us; the launch traced here: 156 us
  blocking collectives  101 us (64%)
  other arithmetic  17.8 us (11%)
  matrix products  12.7 us (8%)
  starting transfers between devices  12.1 us (8%)
  local copies, waits for them, and re-layouts  10.6 us (7%)
  between operations  2.05 us (1%)
    all_gather x1, blocking collectives, turned_gather(): result, at, done = (lax.all_gather(both, axis, axis=0, tiled=True), 0, [])  62.9 us
    psum x4, blocking collectives, by_axis(): array = lax.psum(array, axis)  38 us
    all_to_all x1, starting transfers between devices, local(): lax.all_to_all(genotypes, SAMP, split_axis=1, concat_axis=0, tiled=True)  12.1 us
    dot_general x1, matrix products, block_grams(): jnp.einsum('sbu,sbv->buv', stacked, stacked, preferred_element_type=jnp.f...  8.1 us
    dot_general x1, other arithmetic, block_grams(): jnp.einsum('sbu,sbv->buv', stacked, stacked, preferred_element_type=jnp.f...  6.58 us
    dot_general x1, matrix products, local(): jnp.dot(weighted_residual.reshape(1, -1), flattened, preferred_element_ty...  3.91 us
    another operation x1, local copies, waits for them, and re-layouts, block_stats(): return jnp.stack([burden_sum, burden_var, skat_sum, trace_one, trace_two])  3.27 us
  transfers between devices with their start and end apart: 1, of which 0 were waited for; matrix products, arithmetic and copies ran while one was open for 7% of the time, Pallas kernels for 0%

commit v1 on v0

--- a/solution.py
+++ b/solution.py
@@ -22,7 +22,7 @@
 
 def by_axis(array, axes):
     for axis in axes:
-        array = lax.psum(array, axis)
+        array = jnp.sum(lax.all_gather(array, axis), axis=0)
     return array
 
 

time: 157 us -> 171 us (1.089)
  blocking collectives: 101 us -> 114 us
    all_gather x0 -> x4, blocking collectives: none -> 50.9 us  [by_axis(): array = jnp.sum(lax.all_gather(array, axis), axis=0)]
    psum x4 -> x0, blocking collectives: 38 us -> none  [by_axis(): array = lax.psum(array, axis)]
where the time goes in v1:
time: 171 us; the launch traced here: 169 us
  blocking collectives  114 us (67%)
  other arithmetic  17.8 us (10%)
  matrix products  12.7 us (7%)
  starting transfers between devices  12.1 us (7%)
  local copies, waits for them, and re-layouts  10.6 us (6%)
  between operations  2.05 us (1%)
    all_gather x1, blocking collectives, turned_gather(): result, at, done = (lax.all_gather(both, axis, axis=0, tiled=True), 0, [])  62.9 us
    all_gather x4, blocking collectives, by_axis(): array = jnp.sum(lax.all_gather(array, axis), axis=0)  50.9 us
    all_to_all x1, starting transfers between devices, local(): lax.all_to_all(genotypes, SAMP, split_axis=1, concat_axis=0, tiled=True)  12.1 us
    dot_general x1, matrix products, block_grams(): jnp.einsum('sbu,sbv->buv', stacked, stacked, preferred_element_type=jnp.f...  8.1 us
    dot_general x1, other arithmetic, block_grams(): jnp.einsum('sbu,sbv->buv', stacked, stacked, preferred_element_type=jnp.f...  6.58 us
    dot_general x1, matrix products, local(): jnp.dot(weighted_residual.reshape(1, -1), flattened, preferred_element_ty...  3.91 us
  transfers between devices with their start and end apart: 1, of which 0 were waited for; matrix products, arithmetic and copies ran while one was open for 7% of the time, Pallas kernels for 0%

profile of v1, /device:TPU:8, one launch (start us, length us, event | category | flops | bytes accessed | tf_op | source)
XLA Modules:
  0.0 169.1 jit_solution(11221003486202392358)
XLA Ops:
  0.6 0.0 copy-start
  0.6 0.0 copy-start.1
  0.7 1.2 copy-done
  1.9 1.1 copy_bitcast_fusion
  3.0 12.1 %all-to-all-start = ((s32[32,64,128]{2,0,1:T(8,128)}), s32[32,64,128]{2,0,1:T(8,128)S(1)}, u32[]{:S(2)}, u32[]{:S(2)}) async-start(s32[32,64,128]{2,0,1:T(8,128)} %copy_bitcast_fusion), calls=%async_computation | async-start | bytes 2097152 | tf_op jit(solution)/shard_map/all_to_all | solution.py:83
  15.1 1.3 fusion.19
  16.4 2.0 %fusion.20 = s32[]{:T(128)} fusion(s32[256]{0:T(256)} %param.12, s32[]{:T(128)} %fusion.19), kind=kLoop, calls=%fused_computation.36 | loop fusion | flops 767 | bytes 1032 | tf_op jit(solution)/shard_map/reduce_sum | solution.py:60
  19.1 0.8 copy.15
  19.8 0.8 copy.16
  20.6 0.1 pad_maximum_fusion
  20.7 62.9 %all_gather.27 = f32[2048,32]{1,0:T(8,128)S(1)} all-gather(f32[32,32]{1,0:T(8,128)S(1)} %pad_maximum_fusion), channel_id=1, replica_groups=mesh['samp_0'=4,'samp_1'=8,'samp_2'=2,'gene'=4] {'samp_0','samp_1','samp..., dimensions={0}, use_global_device_ids=true | all-gather | bytes 266240 | tf_op jit(solution)/shard_map/all_gather | solution.py:15
  83.6 1.9 %fusion.15 = (f32[]{:T(128)}, bf16[16,2048,1]{0,1,2:T(8,128)(2,1)}, f32[16,2048]{0,1:T(8,128)S(1)}) fusion(f32[2048,32]{1,0:T(8,128)S(1)} %all_gather.27), kind=kLoop, calls=%fused_computation.19 | loop fusion | flops 163839 | bytes 458756 | tf_op jit(solution)/shard_map/reduce_sum | solution.py:96
  85.5 1.4 copy.21
  86.9 0.3 copy.17
  87.8 0.7 fusion.22
  88.5 0.8 dynamic-slice_multiply_fusion
  89.3 0.0 copy-done.1
  89.3 1.3 fusion.21
  90.6 0.0 all-to-all-done
  90.6 0.3 copy.19
  90.9 6.6 %multiply_convert_fusion.14 = bf16[16,2048,128]{1,2,0:T(8,128)(2,1)} fusion(f32[128]{0:T(128)S(1)} %dynamic-slice_multiply_fusion, s32[16]{0:T(128)S(1)} %iota_multiply_fusion, s32[2048,128]{0,1:T(8,128)S(1)} %copy.19, f32[16,2048]{1,0:T(8,128)S(1)} %copy.17), kind=kLoop, calls=%fused_computation.1.clone.clone.clone.clone.2 | loop fusion | flops 25165824 | bytes 9568832 | tf_op jit(solution)/shard_map/sbu,sbv->buv/dot_general | solution.py:39
  97.5 8.1 %fusion.12 = f32[128,128]{1,0:T(8,128)S(1)} fusion(bf16[16,2048,128]{1,2,0:T(8,128)(2,1)} %multiply_convert_fusion.14), kind=kOutput, calls=%fused_computation.15 | convolution fusion | flops 1073741824 | bytes 8454144 | tf_op jit(solution)/shard_map/sbu,sbv->buv/dot_general | solution.py:39
  105.6 1.4 gather_fusion
  107.0 1.9 %fusion.23 = (f32[]{:T(128)}, f32[1,128]{1,0:T(1,128)S(1)}) fusion(f32[128]{0:T(128)S(1)} %gather_fusion, f32[64,128]{1,0:T(8,128)} %bitcast.78, s32[]{:T(128)S(6)} %select_n.22, s32[]{:T(128)} %fusion.21, s32[]{:T(128)S(6)} %mul.117), kind=kLoop, calls=%fused_computation.40 | loop fusion | flops 767 | bytes 1552 | tf_op jit(solution)/shard_map/reduce_sum | solution.py:49
  109.0 0.7 fusion.17
  109.7 3.9 %multiply_reduce_fusion.1 = (f32[]{:T(128)}, f32[]{:T(128)}) fusion(f32[1,128]{1,0:T(1,128)S(1)} %get-tuple-element.5, bf16[16,2048,1]{1,2,0:T(2,128)(2,1)S(1)} %copy.21, f32[128]{0:T(128)S(1)} %dynamic-slice_multiply_fusion, s32[16]{0:T(128)S(1)} %iota_multiply_fusion, s32[2048,128]{0,1:T(8,128)S(1)} %copy.19, f32[16,2048]{1,0:T(8,128)S(1)} %copy.17), kind=kOutput, calls=%fused_computation.45 | convolution fusion | flops 33554944 | bytes 1246280 | tf_op jit(solution)/shard_map/dot_general | solution.py:93
  113.6 0.7 multiply_reduce_fusion
  114.3 3.3 %stack.23 = f32[5,1]{0,1:T(1,128)S(1)} concatenate(f32[1,1]{0,1:T(1,128)} %bitcast.10, f32[1,1]{0,1:T(1,128)} %bitcast.15, f32[1,1]{0,1:T(1,128)} %bitcast.16, f32[1,1]{0,1:T(1,128)} %bitcast.19, f32[1,1]{0,1:T(1,128)} %bitcast.20), dimensions={0} | concatenate | bytes 40 | tf_op jit(solution)/shard_map/stack | solution.py:52
  117.6 0.1 multiply_bitcast_fusion
  117.7 12.0 %all-gather.4 = f32[4,5,128]{2,1,0:T(8,128)S(1)} all-gather(f32[1,5,128]{2,1,0:T(8,128)S(1)} %multiply_bitcast_fusion), channel_id=2, replica_groups=mesh['samp_0'=4,'samp_1'=8,'samp_2'=2,'gene'=4] {'samp_0'}, dimensions={0}, use_global_device_ids=true | all-gather | bytes 12800 | tf_op jit(solution)/shard_map/all_gather | solution.py:25
  129.7 24.7 %all-gather.5 = f32[8,5,128]{2,1,0:T(8,128)S(1)} all-gather(f32[1,5,128]{2,1,0:T(8,128)S(1)} %bitcast.75), channel_id=3, replica_groups=mesh['samp_0'=4,'samp_1'=8,'samp_2'=2,'gene'=4] {'samp_1'}, dimensions={0}, use_global_device_ids=true | all-gather | bytes 23040 | tf_op jit(solution)/shard_map/all_gather | solution.py:25
  154.4 1.8 %all-gather.6 = f32[2,5,128]{2,1,0:T(8,128)S(1)} all-gather(f32[1,5,128]{2,1,0:T(8,128)S(1)} %bitcast.73), channel_id=4, replica_groups=mesh['samp_0'=4,'samp_1'=8,'samp_2'=2,'gene'=4] {'samp_2'}, dimensions={0}, use_global_device_ids=true | all-gather | bytes 7680 | tf_op jit(solution)/shard_map/all_gather | solution.py:25
  156.2 12.4 %all-gather.7 = f32[4,5,128]{2,1,0:T(8,128)S(1)} all-gather(f32[1,5,128]{2,1,0:T(8,128)S(1)} %bitcast.74), channel_id=5, replica_groups=mesh['samp_0'=4,'samp_1'=8,'samp_2'=2,'gene'=4] {'gene'}, dimensions={0}, use_global_device_ids=true | all-gather | bytes 12800 | tf_op jit(solution)/shard_map/all_gather | solution.py:25
  168.6 0.5 fusion.25
  (6 shorter events, 0.0 us)
Async XLA Ops:
  0.6 1.2 copy-start
  0.6 88.6 %copy-start.1 = (s32[128]{0:T(128)S(1)}, s32[128]{0:T(128)}, u32[]{:S(2)}) copy-start(s32[128]{0:T(128)} %param.13) | copy-start | bytes 1540
  3.0 87.6 %all-to-all-start = ((s32[32,64,128]{2,0,1:T(8,128)}), s32[32,64,128]{2,0,1:T(8,128)S(1)}, u32[]{:S(2)}, u32[]{:S(2)}) async-start(s32[32,64,128]{2,0,1:T(8,128)} %copy_bitcast_fusion), calls=%async_computation | async-start | bytes 2097152 | tf_op jit(solution)/shard_map/all_to_all | solution.py:83
